TPU v7x, 32 devices: a whole 2x2x4 slice. The times are simulated.
32 devices in a mesh: leaf: 16 (over z, y, core), top: 2 (over x).
Axes of the slice: x: 2, y: 2, z: 4, core: 2. Of those that a mesh axis runs over, the one named last changes fastest.
Arguments:
- vectors: bfloat16 [2, 16, 768, 512], P('top', 'leaf'), may hold values from -6 to 6
- near_tiles: bfloat16 [2, 16, 8, 768, 768], P('top', 'leaf'), may hold values from -0.078125 to 0.078125
- leaf_basis: bfloat16 [2, 16, 768, 128], P('top', 'leaf'), may hold values from -0.21875 to 0.21875
- transfer: bfloat16 [2, 16, 128, 128], P('top', 'leaf'), may hold values from -0.25 to 0.25
- coupling: bfloat16 [2, 16, 7, 128, 128], P('top', 'leaf'), may hold values from -0.1875 to 0.1875
- top_coupling: bfloat16 [2, 2, 128, 128], P('top'), may hold values from -0.375 to 0.375
- near_list: int32 [2, 16, 8], P('top', 'leaf'), may hold values from -4 to 4, as said below
- far_list: int32 [2, 16, 7], P('top', 'leaf'), may hold values from 0 to 15, as said below
- row_counts: int32 [2, 16], P('top', 'leaf'), may hold values from 384 to 768
Outputs:
- product: float32 [2, 16, 768, 512], P('top', 'leaf')
Inputs may be any that keep to these rules, and one draw needn't show every extreme that they name: `near_list`: each leaf's 8 offsets are distinct; an offset that leads outside the cluster's 16 leaves stands for an absent block. `far_list`: each leaf's entries are distinct positions in its cluster, each more than 4 away from the leaf's own position. `row_counts`: rows at and beyond the count are padding.
All inputs are finite; a program needn't handle non-finite values.
Results may differ from a plain program's by a relative error of at most 0.0045.
Values may be sent and summed in bfloat16 or wider, within the bound.
A program may use at most 128 MiB of HBM per device.

v0:
```python
import jax
import jax.numpy as jnp
from jax import lax
from jax.sharding import PartitionSpec as P

REACH = 4


def passed_along(block, axis, distance):
    devices = range(lax.axis_size(axis))
    route = [(i - distance, i) for i in devices if i - distance in devices]
    return lax.ppermute(block, axis, route)


def body(
    vectors,
    near_tiles,
    leaf_basis,
    transfer,
    coupling,
    top_coupling,
    near_list,
    far_list,
    row_counts,
):
    leaf_rows = vectors.shape[2]
    row_index = jnp.arange(leaf_rows, dtype=jnp.int32)
    keep = (row_index < row_counts[0, 0]).astype(jnp.bfloat16)
    masked = vectors[0, 0] * keep[:, None]
    offsets = near_list[0, 0]
    tiles = near_tiles[0, 0]
    window = []
    for offset in range(-REACH, REACH + 1):
        if offset == 0:
            window.append(masked)
        else:
            window.append(passed_along(masked, "leaf", -offset))
    stacked = jnp.stack(window)
    span = jnp.arange(-REACH, REACH + 1, dtype=jnp.int32)
    picker = (offsets[:, None] == span[None, :]).astype(jnp.bfloat16)
    sources = jnp.einsum("kw,wrv->krv", picker, stacked, preferred_element_type=jnp.float32)
    near = jnp.einsum(
        "kij,kjv->iv", tiles, sources.astype(jnp.bfloat16), preferred_element_type=jnp.float32
    )
    basis = leaf_basis[0, 0]
    coeff = jnp.einsum("ir,iv->rv", basis, masked, preferred_element_type=jnp.float32).astype(
        jnp.bfloat16
    )
    nested = transfer[0, 0]
    upward = jnp.einsum("ab,av->bv", nested, coeff, preferred_element_type=jnp.float32)
    clusters = lax.axis_size("top")
    owner = (jnp.arange(clusters, dtype=jnp.int32) == lax.axis_index("top")).astype(jnp.float32)
    parents = lax.psum(owner[:, None, None] * upward[None], ("leaf", "top")).astype(jnp.bfloat16)
    sibling_ids = (lax.axis_index("top") + 1 + jnp.arange(clusters, dtype=jnp.int32)) % clusters
    top_pick = (sibling_ids[:, None] == jnp.arange(clusters, dtype=jnp.int32)[None, :]).astype(
        jnp.bfloat16
    )
    chosen = jnp.einsum(
        "mc,crv->mrv", top_pick, parents, preferred_element_type=jnp.float32
    ).astype(jnp.bfloat16)
    parent_field = jnp.einsum(
        "mab,mbv->av", top_coupling[0], chosen, preferred_element_type=jnp.float32
    ).astype(jnp.bfloat16)
    siblings = far_list[0, 0]
    matrices = coupling[0, 0]
    piece = lax.all_gather(coeff[None], "leaf", axis=0, tiled=True)
    blocks = jnp.arange(piece.shape[0], dtype=jnp.int32)
    chooser = (siblings[:, None] == blocks[None, :]).astype(jnp.bfloat16)
    gathered = jnp.einsum("mn,nrv->mrv", chooser, piece, preferred_element_type=jnp.float32).astype(
        jnp.bfloat16
    )
    local_field = jnp.einsum("mab,mbv->av", matrices, gathered, preferred_element_type=jnp.float32)
    local_field = (
        local_field + jnp.dot(nested, parent_field, preferred_element_type=jnp.float32)
    ).astype(jnp.bfloat16)
    result = near + jnp.dot(basis, local_field, preferred_element_type=jnp.float32)
    result = result * keep[:, None].astype(jnp.float32)
    return result[None, None]


def solution(mesh):
    in_specs = (
        P("top", "leaf", None, None),
        P("top", "leaf", None, None, None),
        P("top", "leaf", None, None),
        P("top", "leaf", None, None),
        P("top", "leaf", None, None, None),
        P("top", None, None, None),
        P("top", "leaf", None),
        P("top", "leaf", None),
        P("top", "leaf"),
    )
    out_specs = P("top", "leaf", None, None)
    return jax.shard_map(body, mesh=mesh, in_specs=in_specs, out_specs=out_specs, check_vma=False)
```

profile of v0, /device:TPU:0, one launch (start us, length us, event | category | flops | bytes accessed | tf_op | source)
XLA Modules:
  0.0 217.3 jit_solution(1711316566224805380)
XLA Ops:
  7.3 1.3 bitcast_multiply_fusion.1
  8.6 5.9 %collective-permute-start = (bf16[768,512]{1,0:T(8,128)(2,1)S(1)}, bf16[768,512]{1,0:T(8,128)(2,1)}, u32[]{:S(2)}, u32[]{:S(2)}) collective-permute-start(bf16[768,512]{1,0:T(8,128)(2,1)S(1)} %bitcast_multiply_fusion.1), channel_id=1, source_target_pairs={{0,8},{2,10},{4,12},{6,14},{8,16},{10,18},{12,20},{14,22},{16,24},... | collective-permute-start | bytes 2359304 | tf_op jit(solution)/shard_map/ppermute | solution.py:12
  14.5 3.5 %collective-permute-start.1 = (bf16[768,512]{1,0:T(8,128)(2,1)S(1)}, bf16[768,512]{1,0:T(8,128)(2,1)}, u32[]{:S(2)}, u32[]{:S(2)}) collective-permute-start(bf16[768,512]{1,0:T(8,128)(2,1)S(1)} %bitcast_multiply_fusion.1), channel_id=1, source_target_pairs={{0,6},{2,8},{4,10},{6,12},{8,14},{10,16},{12,18},{14,20},{16,22},{... | collective-permute-start | bytes 2359304 | tf_op jit(solution)/shard_map/ppermute | solution.py:12
  18.0 3.4 %collective-permute-start.2 = (bf16[768,512]{1,0:T(8,128)(2,1)S(1)}, bf16[768,512]{1,0:T(8,128)(2,1)}, u32[]{:S(2)}, u32[]{:S(2)}) collective-permute-start(bf16[768,512]{1,0:T(8,128)(2,1)S(1)} %bitcast_multiply_fusion.1), channel_id=1, source_target_pairs={{0,4},{2,6},{4,8},{6,10},{8,12},{10,14},{12,16},{14,18},{16,20},{1... | collective-permute-start | bytes 2359304 | tf_op jit(solution)/shard_map/ppermute | solution.py:12
  21.4 2.6 %collective-permute-start.3 = (bf16[768,512]{1,0:T(8,128)(2,1)S(1)}, bf16[768,512]{1,0:T(8,128)(2,1)}, u32[]{:S(2)}, u32[]{:S(2)}) collective-permute-start(bf16[768,512]{1,0:T(8,128)(2,1)S(1)} %bitcast_multiply_fusion.1), channel_id=1, source_target_pairs={{0,2},{2,4},{4,6},{6,8},{8,10},{10,12},{12,14},{14,16},{16,18},{18... | collective-permute-start | bytes 2359304 | tf_op jit(solution)/shard_map/ppermute | solution.py:12
  24.0 1.3 collective-permute-start.4
  25.3 2.4 %convolution_convert_fusion = bf16[512,128]{1,0:T(8,128)(2,1)} fusion(bf16[1,1,768,512]{3,2,1,0:T(8,128)(2,1)} %param.9, bf16[768]{0:T(1024)(128)(2,1)S(1)} %fusion.27, bf16[1,1,768,128]{3,2,1,0:T(8,128)(2,1)} %param.11), kind=kOutput, calls=%fused_computation.15 | convolution fusion | flops 101122048 | bytes 1115648 | tf_op jit(solution)/shard_map/ir,iv->rv/dot_general | solution.py:46
  27.7 1.1 convolution_bitcast_fusion.1
  28.9 0.1 broadcast_multiply_fusion
  29.0 86.0 %all-reduce.1 = bf16[2,128,512]{2,1,0:T(8,128)(2,1)S(1)} all-reduce(f32[2,128,512]{2,1,0:T(8,128)S(1)} %broadcast_multiply_fusion), channel_id=1, replica_groups=mesh['leaf'=16,'top'=2] {'leaf','top'}, use_global_device_ids=true, to_apply=%region_0.0 | all-reduce | flops 131072 | bytes 786432 | tf_op jit(solution)/shard_map/psum | solution.py:53
  115.0 0.5 fusion.18
  115.5 1.1 fusion.11
  116.6 1.3 collective-permute-start.5
  117.9 1.2 bitcast_dynamic-update-slice_fusion.7
  119.1 1.3 collective-permute-start.6
  120.4 1.2 bitcast_dynamic-update-slice_fusion.6
  121.6 1.5 collective-permute-start.7
  123.1 1.2 bitcast_dynamic-update-slice_fusion.5
  124.3 1.2 bitcast_dynamic-update-slice_fusion.4
  125.5 0.2 fusion.15
  125.8 13.1 %collective-permute-done.5 = bf16[768,512]{1,0:T(8,128)(2,1)S(1)} collective-permute-done((bf16[768,512]{1,0:T(8,128)(2,1)S(1)}, bf16[768,512]{1,0:T(8,128)(2,1)S(1)}, u32[]{:S(2)}, u32[]{:S(2)}) %collective-permute-start.5) | collective-permute-done | bytes 786464 | tf_op jit(solution)/shard_map/ppermute | solution.py:12
  139.0 5.5 %collective-permute-done.6 = bf16[768,512]{1,0:T(8,128)(2,1)S(1)} collective-permute-done((bf16[768,512]{1,0:T(8,128)(2,1)S(1)}, bf16[768,512]{1,0:T(8,128)(2,1)S(1)}, u32[]{:S(2)}, u32[]{:S(2)}) %collective-permute-start.6) | collective-permute-done | bytes 786464 | tf_op jit(solution)/shard_map/ppermute | solution.py:12
  144.5 26.2 %collective-permute-done.7 = bf16[768,512]{1,0:T(8,128)(2,1)S(1)} collective-permute-done((bf16[768,512]{1,0:T(8,128)(2,1)S(1)}, bf16[768,512]{1,0:T(8,128)(2,1)S(1)}, u32[]{:S(2)}, u32[]{:S(2)}) %collective-permute-start.7) | collective-permute-done | bytes 786464 | tf_op jit(solution)/shard_map/ppermute | solution.py:12
  170.8 8.7 %fusion = bf16[8,768,512]{2,0,1:T(8,128)(2,1)} fusion(bf16[9,768,512]{2,1,0:T(8,128)(2,1)S(1)} %bitcast_dynamic-update-slice_fusion, s32[9]{0:T(128)S(1)} %iota_add_fusion, s32[8]{0:T(128)S(1)} %bitcast.91), kind=kOutput, calls=%fused_computation | convolution fusion | flops 56623176 | bytes 13369412 | tf_op jit(solution)/shard_map/kw,wrv->krv/dot_general | solution.py:41
  179.4 9.1 %copy.12 = bf16[8,768,512]{1,2,0:T(8,128)(2,1)} copy(bf16[8,768,512]{2,0,1:T(8,128)(2,1)} %fusion) | data formatting | bytes 12582912 | tf_op jit(solution)/shard_map/kw,wrv->krv/dot_general | solution.py:41
  188.5 2.3 %copy.17 = bf16[64,8,16,128]{3,2,1,0:T(8,128)(2,1)S(1)} copy(bf16[64,8,16,128]{3,1,2,0:T(8,128)(2,1)} %bitcast.89) | data formatting | bytes 4194304
  190.8 3.6 %copy.13 = bf16[16,128,512]{2,0,1:T(8,128)(2,1)} copy(bf16[16,128,512]{1,0,2:T(8,128)(2,1)S(1)} %bitcast.88) | data formatting | bytes 4194304 | tf_op jit(solution)/shard_map/all_gather | solution.py:66
  194.3 2.1 fusion.29
  196.4 0.6 convolution_bitcast_fusion.2
  197.0 1.7 fusion.13
  198.7 10.2 %fusion.6 = f32[1,1,768,512]{2,3,1,0:T(8,128)S(1)} fusion(f32[512,768]{1,0:T(8,128)} %fusion.13, bf16[1,1,8,768,768]{4,3,2,1,0:T(8,128)(2,1)} %param.10, bf16[8,768,512]{1,2,0:T(8,128)(2,1)} %copy.12, f32[768]{0:T(1024)S(1)} %fusion.37), kind=kOutput, calls=%fused_computation.8 | convolution fusion | flops 4832624640 | bytes 18877440 | tf_op jit(solution)/shard_map/kij,kjv->iv/dot_general | solution.py:42
  208.9 1.6 copy.10
  (29 shorter events, 0.3 us)
Async XLA Ops:
  6.5 189.9 %copy-start = (bf16[1,1,7,128,128]{4,3,2,1,0:T(8,128)(2,1)S(1)}, bf16[1,1,7,128,128]{4,3,2,1,0:T(8,128)(2,1)}, u32[]{:S(2)}) copy-start(bf16[1,1,7,128,128]{4,3,2,1,0:T(8,128)(2,1)} %param.13) | copy-start | bytes 688132
  6.5 119.0 %copy-start.1 = (bf16[1,1,768,512]{3,2,1,0:T(8,128)(2,1)S(1)}, bf16[1,1,768,512]{3,2,1,0:T(8,128)(2,1)}, u32[]{:S(2)}) copy-start(bf16[1,1,768,512]{3,2,1,0:T(8,128)(2,1)} %param.9) | copy-start | bytes 2359300
  6.5 182.0 %all-gather.3.cloned.1.call-start = ((), (), s32[]{:S(2)}) async-start(), calls=%async_computation | async-start | bytes 2228224 | tf_op jit(solution)/shard_map/all_gather | solution.py:66
  8.6 108.0 %collective-permute-start = (bf16[768,512]{1,0:T(8,128)(2,1)S(1)}, bf16[768,512]{1,0:T(8,128)(2,1)}, u32[]{:S(2)}, u32[]{:S(2)}) collective-permute-start(bf16[768,512]{1,0:T(8,128)(2,1)S(1)} %bitcast_multiply_fusion.1), channel_id=1, source_target_pairs={{0,8},{2,10},{4,12},{6,14},{8,16},{10,18},{12,20},{14,22},{16,24},... | collective-permute-start | bytes 2359304 | tf_op jit(solution)/shard_map/ppermute | solution.py:12
  14.5 104.7 %collective-permute-start.1 = (bf16[768,512]{1,0:T(8,128)(2,1)S(1)}, bf16[768,512]{1,0:T(8,128)(2,1)}, u32[]{:S(2)}, u32[]{:S(2)}) collective-permute-start(bf16[768,512]{1,0:T(8,128)(2,1)S(1)} %bitcast_multiply_fusion.1), channel_id=1, source_target_pairs={{0,6},{2,8},{4,10},{6,12},{8,14},{10,16},{12,18},{14,20},{16,22},{... | collective-permute-start | bytes 2359304 | tf_op jit(solution)/shard_map/ppermute | solution.py:12
  18.0 103.6 %collective-permute-start.2 = (bf16[768,512]{1,0:T(8,128)(2,1)S(1)}, bf16[768,512]{1,0:T(8,128)(2,1)}, u32[]{:S(2)}, u32[]{:S(2)}) collective-permute-start(bf16[768,512]{1,0:T(8,128)(2,1)S(1)} %bitcast_multiply_fusion.1), channel_id=1, source_target_pairs={{0,4},{2,6},{4,8},{6,10},{8,12},{10,14},{12,16},{14,18},{16,20},{1... | collective-permute-start | bytes 2359304 | tf_op jit(solution)/shard_map/ppermute | solution.py:12
  21.4 102.9 %collective-permute-start.3 = (bf16[768,512]{1,0:T(8,128)(2,1)S(1)}, bf16[768,512]{1,0:T(8,128)(2,1)}, u32[]{:S(2)}, u32[]{:S(2)}) collective-permute-start(bf16[768,512]{1,0:T(8,128)(2,1)S(1)} %bitcast_multiply_fusion.1), channel_id=1, source_target_pairs={{0,2},{2,4},{4,6},{6,8},{8,10},{10,12},{12,14},{14,16},{16,18},{18... | collective-permute-start | bytes 2359304 | tf_op jit(solution)/shard_map/ppermute | solution.py:12
  24.0 101.8 %collective-permute-start.4 = (bf16[768,512]{1,0:T(8,128)(2,1)S(1)}, bf16[768,512]{1,0:T(8,128)(2,1)S(1)}, u32[]{:S(2)}, u32[]{:S(2)}) collective-permute-start(bf16[768,512]{1,0:T(8,128)(2,1)S(1)} %bitcast_multiply_fusion.1), channel_id=1, source_target_pairs={{2,0},{4,2},{6,4},{8,6},{10,8},{12,10},{14,12},{16,14},{18,16},{20... | collective-permute-start | bytes 2359304 | tf_op jit(solution)/shard_map/ppermute | solution.py:12
  116.6 54.1 %copy-start.4 = (s32[1,1,8]{2,1,0:T(1,128)S(1)}, s32[1,1,8]{2,1,0:T(1,128)}, u32[]{:S(2)}) copy-start(s32[1,1,8]{2,1,0:T(1,128)} %param.15) | copy-start | bytes 100
  116.6 22.3 %collective-permute-start.5 = (bf16[768,512]{1,0:T(8,128)(2,1)S(1)}, bf16[768,512]{1,0:T(8,128)(2,1)S(1)}, u32[]{:S(2)}, u32[]{:S(2)}) collective-permute-start(bf16[768,512]{1,0:T(8,128)(2,1)S(1)} %bitcast_multiply_fusion.1), channel_id=1, source_target_pairs={{4,0},{6,2},{8,4},{10,6},{12,8},{14,10},{16,12},{18,14},{20,16},{2... | collective-permute-start | bytes 2359304 | tf_op jit(solution)/shard_map/ppermute | solution.py:12
  119.1 25.3 %collective-permute-start.6 = (bf16[768,512]{1,0:T(8,128)(2,1)S(1)}, bf16[768,512]{1,0:T(8,128)(2,1)S(1)}, u32[]{:S(2)}, u32[]{:S(2)}) collective-permute-start(bf16[768,512]{1,0:T(8,128)(2,1)S(1)} %bitcast_multiply_fusion.1), channel_id=1, source_target_pairs={{6,0},{8,2},{10,4},{12,6},{14,8},{16,10},{18,12},{20,14},{22,16},{... | collective-permute-start | bytes 2359304 | tf_op jit(solution)/shard_map/ppermute | solution.py:12
  121.6 49.1 %collective-permute-start.7 = (bf16[768,512]{1,0:T(8,128)(2,1)S(1)}, bf16[768,512]{1,0:T(8,128)(2,1)S(1)}, u32[]{:S(2)}, u32[]{:S(2)}) collective-permute-start(bf16[768,512]{1,0:T(8,128)(2,1)S(1)} %bitcast_multiply_fusion.1), channel_id=1, source_target_pairs={{8,0},{10,2},{12,4},{14,6},{16,8},{18,10},{20,12},{22,14},{24,16},... | collective-permute-start | bytes 2359304 | tf_op jit(solution)/shard_map/ppermute | solution.py:12
  188.5 5.9 %copy-start.5 = (s32[1,1,7]{2,1,0:T(1,128)S(1)}, s32[1,1,7]{2,1,0:T(1,128)}, u32[]{:S(2)}) copy-start(s32[1,1,7]{2,1,0:T(1,128)} %param.16) | copy-start | bytes 88
  188.5 8.5 %copy-start.2 = (bf16[1,1,768,128]{3,2,1,0:T(8,128)(2,1)S(1)}, bf16[1,1,768,128]{3,2,1,0:T(8,128)(2,1)}, u32[]{:S(2)}) copy-start(bf16[1,1,768,128]{3,2,1,0:T(8,128)(2,1)} %param.11) | copy-start | bytes 589828
  188.5 8.5 %copy-start.3 = (bf16[1,1,128,128]{3,2,1,0:T(8,128)(2,1)S(1)}, bf16[1,1,128,128]{3,2,1,0:T(8,128)(2,1)}, u32[]{:S(2)}) copy-start(bf16[1,1,128,128]{3,2,1,0:T(8,128)(2,1)} %param.12) | copy-start | bytes 98308
Sparse Core Ops, SparseCore 0:
  27.8 49.3 all-gather.2
where the time goes:
time: 218 us; the launch traced here: 217 us
  blocking collectives  86 us (39%)
  waiting for transfers between devices  44.8 us (21%)
  matrix products  28.3 us (13%)
  local copies, waits for them, and re-layouts  21.5 us (10%)
  starting transfers between devices  20.7 us (9%)
  between operations  14.4 us (7%)
    psum x1, blocking collectives, body(): lax.psum(owner[:, None, None] * upward[None], ('leaf', 'top'))  86 us
    ppermute x8, waiting for transfers between devices, passed_along(): return lax.ppermute(block, axis, route)  44.8 us
    ppermute x8, starting transfers between devices, passed_along(): return lax.ppermute(block, axis, route)  20.7 us
    dot_general x1, matrix products, body(): jnp.einsum('kij,kjv->iv', tiles, sources.astype(jnp.bfloat16), preferred_...  10.2 us
    dot_general x1, local copies, waits for them, and re-layouts, body(): jnp.einsum('kw,wrv->krv', picker, stacked, preferred_element_type=jnp.flo...  9.06 us
    dot_general x1, matrix products, body(): jnp.einsum('kw,wrv->krv', picker, stacked, preferred_element_type=jnp.flo...  8.66 us
    unnamed x20, local copies, waits for them, and re-layouts  7.17 us
  transfers between devices with their start and end apart: 9, of which 3 were waited for; matrix products, arithmetic and copies ran while one was open for 13% of the time, Pallas kernels for 0%

commit v1 on v0

--- a/solution.py
+++ b/solution.py
@@ -50,7 +50,9 @@
     upward = jnp.einsum("ab,av->bv", nested, coeff, preferred_element_type=jnp.float32)
     clusters = lax.axis_size("top")
     owner = (jnp.arange(clusters, dtype=jnp.int32) == lax.axis_index("top")).astype(jnp.float32)
-    parents = lax.psum(owner[:, None, None] * upward[None], ("leaf", "top")).astype(jnp.bfloat16)
+    parents = jnp.sum(
+        lax.all_gather(owner[:, None, None] * upward[None], ("leaf", "top")), axis=0
+    ).astype(jnp.bfloat16)
     sibling_ids = (lax.axis_index("top") + 1 + jnp.arange(clusters, dtype=jnp.int32)) % clusters
     top_pick = (sibling_ids[:, None] == jnp.arange(clusters, dtype=jnp.int32)[None, :]).astype(
         jnp.bfloat16

time: 218 us -> 236 us (1.083)
  waiting for transfers between devices: 44.8 us -> 145 us
  blocking collectives: 86 us -> 0 us
  other arithmetic: 1.67 us -> 10.2 us
  matrix products: 28.3 us -> 25.7 us
    psum x1 -> x0, blocking collectives: 86 us -> none  [body(): lax.psum(owner[:, None, None] * upward[None], ('leaf', 'top'))]
    all_gather x0 -> x1, waiting for transfers between devices: none -> 63.8 us  [body(): lax.all_gather(owner[:, None, None] * upward[None], ('leaf', 'top'))]
    ppermute x8, waiting for transfers between devices: 44.8 us -> 81.1 us  [passed_along(): return lax.ppermute(block, axis, route)]
    reduce_sum x0 -> x1, other arithmetic: none -> 7.73 us  [body(): jnp.sum(lax.all_gather(owner[:, None, None] * upward[None], ('leaf', 'top...]
    unnamed x20 -> x24, local copies, waits for them, and re-layouts: 7.17 us -> 6.02 us
  transfers between devices with their start and end apart: 9 -> 10, of which waited for: 3 -> 5; matrix products, arithmetic and copies ran while one was open for 13% -> 14% of each run, Pallas kernels for 0% -> 0%
where the time goes in v1:
time: 236 us; the launch traced here: 235 us
  waiting for transfers between devices  145 us (61%)
  matrix products  25.7 us (11%)
  local copies, waits for them, and re-layouts  20.5 us (9%)
  starting transfers between devices  19.7 us (8%)
  between operations  14.5 us (6%)
  other arithmetic  10.2 us (4%)
    ppermute x8, waiting for transfers between devices, passed_along(): return lax.ppermute(block, axis, route)  81.1 us
    all_gather x1, waiting for transfers between devices, body(): lax.all_gather(owner[:, None, None] * upward[None], ('leaf', 'top'))  63.8 us
    ppermute x8, starting transfers between devices, passed_along(): return lax.ppermute(block, axis, route)  19.7 us
    dot_general x1, matrix products, body(): jnp.einsum('kij,kjv->iv', tiles, sources.astype(jnp.bfloat16), preferred_...  9.52 us
    dot_general x1, local copies, waits for them, and re-layouts, body(): jnp.einsum('kw,wrv->krv', picker, stacked, preferred_element_type=jnp.flo...  9.24 us
    dot_general x1, matrix products, body(): jnp.einsum('kw,wrv->krv', picker, stacked, preferred_element_type=jnp.flo...  8.7 us
    reduce_sum x1, other arithmetic, body(): jnp.sum(lax.all_gather(owner[:, None, None] * upward[None], ('leaf', 'top...  7.73 us
    unnamed x24, local copies, waits for them, and re-layouts  6.02 us
  transfers between devices with their start and end apart: 10, of which 5 were waited for; matrix products, arithmetic and copies ran while one was open for 14% of the time, Pallas kernels for 0%

profile of v1, /device:TPU:0, one launch (start us, length us, event | category | flops | bytes accessed | tf_op | source)
XLA Modules:
  0.0 235.4 jit_solution(16084770655916595658)
XLA Ops:
  7.3 2.4 %convolution_convert_fusion = bf16[512,128]{1,0:T(8,128)(2,1)} fusion(bf16[1,1,768,512]{3,2,1,0:T(8,128)(2,1)} %param.9, bf16[768]{0:T(1024)(128)(2,1)S(1)} %fusion.27, bf16[1,1,768,128]{3,2,1,0:T(8,128)(2,1)} %param.11), kind=kOutput, calls=%fused_computation.15 | convolution fusion | flops 101122048 | bytes 1115648 | tf_op jit(solution)/shard_map/ir,iv->rv/dot_general | solution.py:46
  9.8 1.1 convolution_bitcast_fusion.1
  10.9 0.9 broadcast_multiply_fusion
  11.9 1.3 bitcast_multiply_fusion.1
  13.2 5.9 %collective-permute-start = (bf16[768,512]{1,0:T(8,128)(2,1)S(1)}, bf16[768,512]{1,0:T(8,128)(2,1)}, u32[]{:S(2)}, u32[]{:S(2)}) collective-permute-start(bf16[768,512]{1,0:T(8,128)(2,1)S(1)} %bitcast_multiply_fusion.1), channel_id=1, source_target_pairs={{0,8},{2,10},{4,12},{6,14},{8,16},{10,18},{12,20},{14,22},{16,24},... | collective-permute-start | bytes 2359304 | tf_op jit(solution)/shard_map/ppermute | solution.py:12
  19.0 3.5 %collective-permute-start.1 = (bf16[768,512]{1,0:T(8,128)(2,1)S(1)}, bf16[768,512]{1,0:T(8,128)(2,1)}, u32[]{:S(2)}, u32[]{:S(2)}) collective-permute-start(bf16[768,512]{1,0:T(8,128)(2,1)S(1)} %bitcast_multiply_fusion.1), channel_id=1, source_target_pairs={{0,6},{2,8},{4,10},{6,12},{8,14},{10,16},{12,18},{14,20},{16,22},{... | collective-permute-start | bytes 2359304 | tf_op jit(solution)/shard_map/ppermute | solution.py:12
  22.5 3.4 %collective-permute-start.2 = (bf16[768,512]{1,0:T(8,128)(2,1)S(1)}, bf16[768,512]{1,0:T(8,128)(2,1)}, u32[]{:S(2)}, u32[]{:S(2)}) collective-permute-start(bf16[768,512]{1,0:T(8,128)(2,1)S(1)} %bitcast_multiply_fusion.1), channel_id=1, source_target_pairs={{0,4},{2,6},{4,8},{6,10},{8,12},{10,14},{12,16},{14,18},{16,20},{1... | collective-permute-start | bytes 2359304 | tf_op jit(solution)/shard_map/ppermute | solution.py:12
  25.9 1.8 collective-permute-start.3
  27.7 1.3 collective-permute-start.4
  29.1 11.9 %collective-permute-done = bf16[768,512]{1,0:T(8,128)(2,1)} collective-permute-done((bf16[768,512]{1,0:T(8,128)(2,1)S(1)}, bf16[768,512]{1,0:T(8,128)(2,1)}, u32[]{:S(2)}, u32[]{:S(2)}) %collective-permute-start) | collective-permute-done | bytes 786464 | tf_op jit(solution)/shard_map/ppermute | solution.py:12
  41.0 1.3 collective-permute-start.5
  42.3 1.2 bitcast_dynamic-update-slice_fusion.7
  43.5 13.9 %collective-permute-done.1 = bf16[768,512]{1,0:T(8,128)(2,1)} collective-permute-done((bf16[768,512]{1,0:T(8,128)(2,1)S(1)}, bf16[768,512]{1,0:T(8,128)(2,1)}, u32[]{:S(2)}, u32[]{:S(2)}) %collective-permute-start.1) | collective-permute-done | bytes 786464 | tf_op jit(solution)/shard_map/ppermute | solution.py:12
  57.4 1.3 collective-permute-start.6
  58.7 1.2 bitcast_dynamic-update-slice_fusion.6
  59.8 33.2 %collective-permute-done.2 = bf16[768,512]{1,0:T(8,128)(2,1)} collective-permute-done((bf16[768,512]{1,0:T(8,128)(2,1)S(1)}, bf16[768,512]{1,0:T(8,128)(2,1)}, u32[]{:S(2)}, u32[]{:S(2)}) %collective-permute-start.2) | collective-permute-done | bytes 786464 | tf_op jit(solution)/shard_map/ppermute | solution.py:12
  93.1 1.3 collective-permute-start.7
  94.4 1.2 bitcast_dynamic-update-slice_fusion.5
  96.1 22.1 %collective-permute-done.7 = bf16[768,512]{1,0:T(8,128)(2,1)S(1)} collective-permute-done((bf16[768,512]{1,0:T(8,128)(2,1)S(1)}, bf16[768,512]{1,0:T(8,128)(2,1)S(1)}, u32[]{:S(2)}, u32[]{:S(2)}) %collective-permute-start.7) | collective-permute-done | bytes 786464 | tf_op jit(solution)/shard_map/ppermute | solution.py:12
  118.2 8.7 %fusion = bf16[8,768,512]{2,0,1:T(8,128)(2,1)} fusion(bf16[9,768,512]{2,1,0:T(8,128)(2,1)S(1)} %bitcast_dynamic-update-slice_fusion, s32[9]{0:T(128)S(1)} %iota_add_fusion, s32[8]{0:T(128)S(1)} %bitcast.91), kind=kOutput, calls=%fused_computation | convolution fusion | flops 56623176 | bytes 13369412 | tf_op jit(solution)/shard_map/kw,wrv->krv/dot_general | solution.py:41
  126.9 9.2 %copy.13 = bf16[8,768,512]{1,2,0:T(8,128)(2,1)} copy(bf16[8,768,512]{2,0,1:T(8,128)(2,1)} %fusion) | data formatting | bytes 12582912 | tf_op jit(solution)/shard_map/kw,wrv->krv/dot_general | solution.py:41
  136.2 2.2 copy.18
  138.4 3.5 %copy.14 = bf16[16,128,512]{2,0,1:T(8,128)(2,1)} copy(bf16[16,128,512]{1,0,2:T(8,128)(2,1)S(1)} %bitcast.88) | data formatting | bytes 4194304 | tf_op jit(solution)/shard_map/all_gather | solution.py:68
  141.9 2.1 fusion.29
  144.0 0.6 convolution_bitcast_fusion.2
  144.6 63.8 %all-gather.4.cloned.1.call-done = f32[32,2,128,512]{3,2,1,0:T(8,128)} async-done(((f32[1,2,128,512]{3,2,1,0:T(8,128)}), f32[32,2,128,512]{3,2,1,0:T(8,128)}) %all-gather.4.cloned.1.call-update) | async-done | bytes 16777232 | tf_op jit(solution)/shard_map/all_gather | solution.py:54
  208.4 7.7 %reduce_sum.9 = bf16[2,128,512]{2,1,0:T(8,128)(2,1)S(1)} reduce(f32[32,2,128,512]{3,2,1,0:T(8,128)} %all-gather.4.cloned.1.call-done, f32[]{:T(128)} %constant.23.clone.1), dimensions={0}, to_apply=%region_0.0 | reduce | flops 4063232 | bytes 17039364 | tf_op jit(solution)/shard_map/reduce_sum | solution.py:53
  216.1 0.5 fusion.18
  216.6 0.3 fusion.11
  216.9 0.5 fusion.13
  217.5 9.5 %fusion.6 = f32[1,1,768,512]{2,3,1,0:T(8,128)S(1)} fusion(f32[512,768]{1,0:T(8,128)S(1)} %fusion.13, bf16[1,1,8,768,768]{4,3,2,1,0:T(8,128)(2,1)} %param.10, bf16[8,768,512]{1,2,0:T(8,128)(2,1)} %copy.13, f32[768]{0:T(1024)S(1)} %fusion.37), kind=kOutput, calls=%fused_computation.8 | convolution fusion | flops 4832624640 | bytes 18877440 | tf_op jit(solution)/shard_map/kij,kjv->iv/dot_general | solution.py:42
  227.0 1.6 copy.11
  (36 shorter events, 0.6 us)
Async XLA Ops:
  6.5 137.5 %copy-start = (bf16[1,1,7,128,128]{4,3,2,1,0:T(8,128)(2,1)S(1)}, bf16[1,1,7,128,128]{4,3,2,1,0:T(8,128)(2,1)}, u32[]{:S(2)}) copy-start(bf16[1,1,7,128,128]{4,3,2,1,0:T(8,128)(2,1)} %param.13) | copy-start | bytes 688132
  6.5 89.1 %copy-start.2 = (bf16[1,1,768,512]{3,2,1,0:T(8,128)(2,1)S(1)}, bf16[1,1,768,512]{3,2,1,0:T(8,128)(2,1)}, u32[]{:S(2)}) copy-start(bf16[1,1,768,512]{3,2,1,0:T(8,128)(2,1)} %param.9) | copy-start | bytes 2359300
  6.5 129.6 %all-gather.6.cloned.1.call-start = ((), (), s32[]{:S(2)}) async-start(), calls=%async_computation.1 | async-start | bytes 2228224 | tf_op jit(solution)/shard_map/all_gather | solution.py:68
  9.7 198.7 %all-gather.4.cloned.1.call-start = ((), (), s32[]{:S(2)}) async-start(), calls=%async_computation | async-start | bytes 17301504 | tf_op jit(solution)/shard_map/all_gather | solution.py:54
  13.2 27.8 %collective-permute-start = (bf16[768,512]{1,0:T(8,128)(2,1)S(1)}, bf16[768,512]{1,0:T(8,128)(2,1)}, u32[]{:S(2)}, u32[]{:S(2)}) collective-permute-start(bf16[768,512]{1,0:T(8,128)(2,1)S(1)} %bitcast_multiply_fusion.1), channel_id=1, source_target_pairs={{0,8},{2,10},{4,12},{6,14},{8,16},{10,18},{12,20},{14,22},{16,24},... | collective-permute-start | bytes 2359304 | tf_op jit(solution)/shard_map/ppermute | solution.py:12
  19.0 38.3 %collective-permute-start.1 = (bf16[768,512]{1,0:T(8,128)(2,1)S(1)}, bf16[768,512]{1,0:T(8,128)(2,1)}, u32[]{:S(2)}, u32[]{:S(2)}) collective-permute-start(bf16[768,512]{1,0:T(8,128)(2,1)S(1)} %bitcast_multiply_fusion.1), channel_id=1, source_target_pairs={{0,6},{2,8},{4,10},{6,12},{8,14},{10,16},{12,18},{14,20},{16,22},{... | collective-permute-start | bytes 2359304 | tf_op jit(solution)/shard_map/ppermute | solution.py:12
  22.5 70.6 %collective-permute-start.2 = (bf16[768,512]{1,0:T(8,128)(2,1)S(1)}, bf16[768,512]{1,0:T(8,128)(2,1)}, u32[]{:S(2)}, u32[]{:S(2)}) collective-permute-start(bf16[768,512]{1,0:T(8,128)(2,1)S(1)} %bitcast_multiply_fusion.1), channel_id=1, source_target_pairs={{0,4},{2,6},{4,8},{6,10},{8,12},{10,14},{12,16},{14,18},{16,20},{1... | collective-permute-start | bytes 2359304 | tf_op jit(solution)/shard_map/ppermute | solution.py:12
  25.9 69.6 %collective-permute-start.3 = (bf16[768,512]{1,0:T(8,128)(2,1)S(1)}, bf16[768,512]{1,0:T(8,128)(2,1)S(1)}, u32[]{:S(2)}, u32[]{:S(2)}) collective-permute-start(bf16[768,512]{1,0:T(8,128)(2,1)S(1)} %bitcast_multiply_fusion.1), channel_id=1, source_target_pairs={{0,2},{2,4},{4,6},{6,8},{8,10},{10,12},{12,14},{14,16},{16,18},{18... | collective-permute-start | bytes 2359304 | tf_op jit(solution)/shard_map/ppermute | solution.py:12
  27.7 68.2 %collective-permute-start.4 = (bf16[768,512]{1,0:T(8,128)(2,1)S(1)}, bf16[768,512]{1,0:T(8,128)(2,1)S(1)}, u32[]{:S(2)}, u32[]{:S(2)}) collective-permute-start(bf16[768,512]{1,0:T(8,128)(2,1)S(1)} %bitcast_multiply_fusion.1), channel_id=1, source_target_pairs={{2,0},{4,2},{6,4},{8,6},{10,8},{12,10},{14,12},{16,14},{18,16},{20... | collective-permute-start | bytes 2359304 | tf_op jit(solution)/shard_map/ppermute | solution.py:12
  29.1 89.1 %copy-start.6 = (s32[1,1,8]{2,1,0:T(1,128)S(1)}, s32[1,1,8]{2,1,0:T(1,128)}, u32[]{:S(2)}) copy-start(s32[1,1,8]{2,1,0:T(1,128)} %param.15) | copy-start | bytes 100
  41.0 54.9 %collective-permute-start.5 = (bf16[768,512]{1,0:T(8,128)(2,1)S(1)}, bf16[768,512]{1,0:T(8,128)(2,1)S(1)}, u32[]{:S(2)}, u32[]{:S(2)}) collective-permute-start(bf16[768,512]{1,0:T(8,128)(2,1)S(1)} %bitcast_multiply_fusion.1), channel_id=1, source_target_pairs={{4,0},{6,2},{8,4},{10,6},{12,8},{14,10},{16,12},{18,14},{20,16},{2... | collective-permute-start | bytes 2359304 | tf_op jit(solution)/shard_map/ppermute | solution.py:12
  57.4 38.7 %collective-permute-start.6 = (bf16[768,512]{1,0:T(8,128)(2,1)S(1)}, bf16[768,512]{1,0:T(8,128)(2,1)S(1)}, u32[]{:S(2)}, u32[]{:S(2)}) collective-permute-start(bf16[768,512]{1,0:T(8,128)(2,1)S(1)} %bitcast_multiply_fusion.1), channel_id=1, source_target_pairs={{6,0},{8,2},{10,4},{12,6},{14,8},{16,10},{18,12},{20,14},{22,16},{... | collective-permute-start | bytes 2359304 | tf_op jit(solution)/shard_map/ppermute | solution.py:12
  93.1 25.1 %collective-permute-start.7 = (bf16[768,512]{1,0:T(8,128)(2,1)S(1)}, bf16[768,512]{1,0:T(8,128)(2,1)S(1)}, u32[]{:S(2)}, u32[]{:S(2)}) collective-permute-start(bf16[768,512]{1,0:T(8,128)(2,1)S(1)} %bitcast_multiply_fusion.1), channel_id=1, source_target_pairs={{8,0},{10,2},{12,4},{14,6},{16,8},{18,10},{20,12},{22,14},{24,16},... | collective-permute-start | bytes 2359304 | tf_op jit(solution)/shard_map/ppermute | solution.py:12
  136.2 5.8 %copy-start.7 = (s32[1,1,7]{2,1,0:T(1,128)S(1)}, s32[1,1,7]{2,1,0:T(1,128)}, u32[]{:S(2)}) copy-start(s32[1,1,7]{2,1,0:T(1,128)} %param.16) | copy-start | bytes 88
  144.6 72.0 %copy-start.5 = (bf16[1,2,128,128]{3,2,1,0:T(8,128)(2,1)S(1)}, bf16[1,2,128,128]{3,2,1,0:T(8,128)(2,1)}, u32[]{:S(2)}) copy-start(bf16[1,2,128,128]{3,2,1,0:T(8,128)(2,1)} %param.14) | copy-start | bytes 196612
  144.6 72.3 %copy-start.3 = (bf16[1,1,768,128]{3,2,1,0:T(8,128)(2,1)S(1)}, bf16[1,1,768,128]{3,2,1,0:T(8,128)(2,1)}, u32[]{:S(2)}) copy-start(bf16[1,1,768,128]{3,2,1,0:T(8,128)(2,1)} %param.11) | copy-start | bytes 589828
  144.6 72.3 %copy-start.4 = (bf16[1,1,128,128]{3,2,1,0:T(8,128)(2,1)S(1)}, bf16[1,1,128,128]{3,2,1,0:T(8,128)(2,1)}, u32[]{:S(2)}) copy-start(bf16[1,1,128,128]{3,2,1,0:T(8,128)(2,1)} %param.12) | copy-start | bytes 98308
  217.5 11.2 %copy-start.1 = (bf16[1,1,7,128,128]{4,3,2,1,0:T(8,128)(2,1)S(1)}, bf16[1,1,7,128,128]{4,3,2,1,0:T(8,128)(2,1)}, u32[]{:S(2)}) copy-start(bf16[1,1,7,128,128]{4,3,2,1,0:T(8,128)(2,1)} %param.13) | copy-start | bytes 688132
Sparse Core Ops, SparseCore 0:
  9.8 59.8 all-gather.5
  72.7 135.6 all-gather.3
